TPU v7x, 32 devices: a whole 2x2x4 slice. The times are simulated.
32 devices in a mesh: grp: 2 (over y), zt: 4 (over x, core), xy: 4 (over z).
Axes of the slice: x: 2, y: 2, z: 4, core: 2. Of those that a mesh axis runs over, the one named last changes fastest.
Arguments:
- source: float32 [2, 2, 3, 8, 16, 128], P('grp', None, None, 'xy', 'zt'), may hold values from -6 to 6
- links: float32 [4, 2, 3, 3, 8, 16, 128], P('grp', None, None, None, 'xy', 'zt'), may hold values from -2 to 2
- shifts: float32 [12], replicated, may hold values from 0.01 to 0.5
- residues: float32 [12], replicated, may hold values from 0.05 to 0.5
- mass: float32 [1], replicated, may hold values from 0.1 to 0.5
Outputs:
- rational: float32 [2, 2, 3, 8, 16, 128], P('grp', None, None, 'xy', 'zt')
- action: float32 [1], replicated
All inputs are finite; a program needn't handle non-finite values.
Results may differ from a plain program's by a relative error of at most 0.0003.
Values sent between devices are 32-bit elements; how exact they have to be, the bound alone decides.
A program may use at most 64 MiB of HBM per device.

v0:
```python
import jax
import jax.numpy as jnp
from jax import lax
from jax.sharding import PartitionSpec as P

NY = 2
NZ = 64
ITERS = 8


def shifted(block, axis, distance):
    devices = range(lax.axis_size(axis))
    route = [((i - distance) % len(devices), i) for i in devices]
    return lax.ppermute(block, axis, route)


def extended(block, sides, width):
    for axis, dim in sides:
        count = lax.axis_size(axis)
        forward = [(i, i + 1) for i in range(count - 1)]
        forward.append((count - 1, 0))
        backward = [(target, source) for source, target in forward]
        low = lax.ppermute(
            lax.slice_in_dim(block, block.shape[dim] - width, None, axis=dim), axis, forward
        )
        high = lax.ppermute(lax.slice_in_dim(block, 0, width, axis=dim), axis, backward)
        block = jnp.concatenate([low, block, high], axis=dim)
    return block


def sign_of(values):
    return (1 - 2 * (values % 2)).astype(jnp.float32)


def phases(coord_x, coord_t, last_t):
    yz_index = jnp.arange(NY * NZ, dtype=jnp.int32)
    ycoord = yz_index // NZ
    zcoord = yz_index % NZ
    unity = jnp.ones((coord_x.shape[0], coord_t.shape[0], NY * NZ), jnp.float32)
    boundary = jnp.where(coord_t == last_t, -1.0, 1.0).astype(jnp.float32)
    eta_y = sign_of(coord_x)[:, None, None] * unity
    eta_z = sign_of(coord_x[:, None, None] + ycoord[None, None, :]) * unity
    eta_t = (
        sign_of(coord_x[:, None, None] + ycoord[None, None, :] + zcoord[None, None, :])
        * boundary[None, :, None]
    )
    return jnp.stack([unity, eta_y, eta_z, eta_t])


def times_link(link, field):
    real = jnp.sum(
        link[0][None] * field[:, 0][:, None] - link[1][None] * field[:, 1][:, None], axis=2
    )
    imag = jnp.sum(
        link[0][None] * field[:, 1][:, None] + link[1][None] * field[:, 0][:, None], axis=2
    )
    return jnp.stack([real, imag], axis=1)


def times_adjoint(link, field):
    real = jnp.sum(
        link[0][None] * field[:, 0][:, :, None] + link[1][None] * field[:, 1][:, :, None], axis=1
    )
    imag = jnp.sum(
        link[0][None] * field[:, 1][:, :, None] - link[1][None] * field[:, 0][:, :, None], axis=1
    )
    return jnp.stack([real, imag], axis=1)


def roll_ycoord(values, offset):
    return jnp.roll(values, offset * NZ, axis=-1)


def roll_zcoord(values, offset):
    shape = values.shape
    return jnp.roll(values.reshape(shape[:-1] + (NY, NZ)), offset, axis=-1).reshape(shape)


def hopping(field, link):
    inner_field = field[..., 1:-1, 1:-1, :]
    inner_link = link[..., 1:-1, 1:-1, :]
    total = times_link(inner_link[0], field[..., 2:, 1:-1, :]) - times_adjoint(
        link[0][..., :-2, 1:-1, :], field[..., :-2, 1:-1, :]
    )
    total = (
        total
        + times_link(inner_link[1], roll_ycoord(inner_field, -1))
        - roll_ycoord(times_adjoint(inner_link[1], inner_field), 1)
    )
    total = (
        total
        + times_link(inner_link[2], roll_zcoord(inner_field, -1))
        - roll_zcoord(times_adjoint(inner_link[2], inner_field), 1)
    )
    total = (
        total
        + times_link(inner_link[3], field[..., 1:-1, 2:, :])
        - times_adjoint(link[3][..., 1:-1, :-2, :], field[..., 1:-1, :-2, :])
    )
    return 0.5 * total


def local_dot(left, right):
    return jnp.sum(left * right, axis=(1, 2, 3, 4, 5))


def spread(values):
    return values.reshape(values.shape + (1, 1, 1, 1, 1))


def on_device(source, links, shifts, residues, mass):
    all_links = lax.all_gather(links, "grp", axis=0, tiled=True)
    cells_x = source.shape[3]
    cells_t = source.shape[4]
    coord_x = lax.axis_index("xy") * cells_x + jnp.arange(cells_x, dtype=jnp.int32)
    coord_t = lax.axis_index("zt") * cells_t + jnp.arange(cells_t, dtype=jnp.int32)
    eta = phases(coord_x, coord_t, cells_t * lax.axis_size("zt") - 1)
    folded = all_links * eta[:, None, None, None]
    mass_sq = mass[0] * mass[0]
    rim_x = shifted(folded[0][:, :, :, -1:, :, :], "xy", 1)
    rim_t = shifted(folded[3][:, :, :, :, -1:, :], "zt", 1)
    wide_links = jnp.pad(folded, ((0, 0), (0, 0), (0, 0), (0, 0), (1, 1), (1, 1), (0, 0)))
    wide_links = wide_links.at[0, :, :, :, 0:1, 1:-1, :].set(rim_x)
    wide_links = wide_links.at[3, :, :, :, 1:-1, 0:1, :].set(rim_t)

    def with_faces(field):
        return extended(field, (("zt", 4), ("xy", 3)), 1)

    shift_col = shifts[:, None]
    members = source.shape[0]
    residual = source
    direction = source
    solutions = jnp.zeros((shifts.shape[0],) + source.shape, jnp.float32)
    directions = jnp.broadcast_to(source[None], solutions.shape)
    norm_now = lax.psum(local_dot(source, source), ("zt", "xy"))
    zeta_now = jnp.ones((shifts.shape[0], members), jnp.float32)
    zeta_old = jnp.ones((shifts.shape[0], members), jnp.float32)
    alpha_old = jnp.ones((members,), jnp.float32)
    beta_old = jnp.zeros((members,), jnp.float32)
    for iteration in range(ITERS):
        first_hop = hopping(with_faces(direction), wide_links)
        image = mass_sq * direction - hopping(with_faces(first_hop), wide_links)
        curvature_sum, cross_sum, image_sum = lax.psum(
            (local_dot(direction, image), local_dot(residual, image), local_dot(image, image)),
            ("zt", "xy"),
        )
        alpha_now = norm_now / curvature_sum
        zeta_new = (
            zeta_now
            * zeta_old
            * alpha_old
            / (
                alpha_now * beta_old * (zeta_old - zeta_now)
                + zeta_old * alpha_old * (1.0 + shift_col * alpha_now)
            )
        )
        alpha_shift = alpha_now * zeta_new / zeta_now
        solutions = solutions + spread(alpha_shift) * directions
        if iteration + 1 < ITERS:
            residual = residual - spread(alpha_now) * image
            norm_next = norm_now - 2.0 * alpha_now * cross_sum + alpha_now * alpha_now * image_sum
            beta_now = norm_next / norm_now
            beta_shift = beta_now * (zeta_new / zeta_now) ** 2
            direction = residual + spread(beta_now) * direction
            directions = spread(zeta_new) * residual[None] + spread(beta_shift) * directions
            zeta_old = zeta_now
            zeta_now = zeta_new
            alpha_old = alpha_now
            beta_old = beta_now
            norm_now = norm_next
    rational = jnp.sum(residues.reshape((-1, 1, 1, 1, 1, 1, 1)) * solutions, axis=0)
    total = lax.psum(jnp.sum(source * rational), ("grp", "zt", "xy"))
    site_count = (
        members
        * lax.axis_size("grp")
        * cells_x
        * lax.axis_size("xy")
        * cells_t
        * lax.axis_size("zt")
        * NY
        * NZ
    )
    action = (total / site_count).reshape(1)
    return (rational, action)


def solution(mesh):
    placed = (
        P("grp", None, None, "xy", "zt", None),
        P("grp", None, None, None, "xy", "zt", None),
        P(),
        P(),
        P(),
    )
    return jax.shard_map(
        on_device,
        mesh=mesh,
        in_specs=placed,
        out_specs=(P("grp", None, None, "xy", "zt", None), P()),
        check_vma=False,
    )
```

profile of v0, /device:TPU:0, one launch (start us, length us, event | category | flops | bytes accessed | tf_op | source)
XLA Modules:
  0.0 512.2 jit_solution(10780419264730769000)
XLA Ops:
  0.7 7.8 %all_gather.3 = f32[4,2,3,3,2,4,128]{6,5,4,3,2,1,0:T(4,128)S(1)} all-gather(f32[2,2,3,3,2,4,128]{6,5,4,3,2,1,0:T(4,128)} %param.10), channel_id=1, replica_groups=mesh['grp'=2,'zt'=4,'xy'=4] {'grp'}, dimensions={0}, use_global_device_ids=true | all-gather | bytes 442368 | tf_op jit(solution)/shard_map/all_gather | solution.py:112
  8.8 1.8 collective-permute-start
  10.8 1.6 collective-permute-start.2
  14.1 2.1 collective-permute-start.4
  16.3 1.7 collective-permute-done.4
  18.0 3.9 collective-permute-done.5
  24.9 1.6 collective-permute-start.7
  30.0 1.8 collective-permute-done.8
  31.7 2.6 collective-permute-done.9
  36.1 30.7 %all-reduce.7 = (f32[1]{0:T(128)}, f32[1]{0:T(128)}, f32[1]{0:T(128)}) all-reduce(f32[1]{0:T(128)} %bitcast, f32[1]{0:T(128)} %bitcast.76, f32[1]{0:T(128)} %bitcast.80), channel_id=1, replica_groups=mesh['grp'=2,'zt'=4,'xy'=4] {'zt','xy'}, use_global_device_ids=true, to_apply=%region_1.2 | all-reduce | flops 3 | bytes 24 | tf_op jit(solution)/shard_map/psum | solution.py:135
  71.4 1.7 collective-permute-start.11
  76.6 1.8 collective-permute-done.12
  78.4 3.0 collective-permute-done.13
  83.9 1.7 collective-permute-start.15
  87.6 1.5 collective-permute-start.17
  89.1 2.0 collective-permute-done.16
  91.1 2.3 collective-permute-done.17
  95.2 30.6 %all-reduce.6 = (f32[1]{0:T(128)}, f32[1]{0:T(128)}, f32[1]{0:T(128)}) all-reduce(f32[1]{0:T(128)} %bitcast.140, f32[1]{0:T(128)} %bitcast.144, f32[1]{0:T(128)} %bitcast.145), channel_id=1, replica_groups=mesh['grp'=2,'zt'=4,'xy'=4] {'zt','xy'}, use_global_device_ids=true, to_apply=%region_71.72 | all-reduce | flops 3 | bytes 24 | tf_op jit(solution)/shard_map/psum | solution.py:143
  128.4 1.7 collective-permute-start.19
  133.6 1.8 collective-permute-done.20
  135.4 2.8 collective-permute-done.21
  140.7 1.7 collective-permute-start.23
  145.9 1.8 collective-permute-done.24
  147.7 2.5 collective-permute-done.25
  152.0 30.4 %all-reduce.5 = (f32[1]{0:T(128)}, f32[1]{0:T(128)}, f32[1]{0:T(128)}) all-reduce(f32[1]{0:T(128)} %bitcast.205, f32[1]{0:T(128)} %bitcast.209, f32[1]{0:T(128)} %bitcast.210), channel_id=1, replica_groups=mesh['grp'=2,'zt'=4,'xy'=4] {'zt','xy'}, use_global_device_ids=true, to_apply=%region_109.110 | all-reduce | flops 3 | bytes 24 | tf_op jit(solution)/shard_map/psum | solution.py:143
  185.1 1.7 collective-permute-start.27
  190.5 1.7 collective-permute-done.28
  192.2 3.1 collective-permute-done.29
  197.9 1.7 collective-permute-start.31
  201.5 1.5 collective-permute-start.33
  203.0 2.0 collective-permute-done.32
  205.0 2.3 collective-permute-done.33
  209.2 30.6 %all-reduce.4 = (f32[1]{0:T(128)}, f32[1]{0:T(128)}, f32[1]{0:T(128)}) all-reduce(f32[1]{0:T(128)} %bitcast.270, f32[1]{0:T(128)} %bitcast.274, f32[1]{0:T(128)} %bitcast.275), channel_id=1, replica_groups=mesh['grp'=2,'zt'=4,'xy'=4] {'zt','xy'}, use_global_device_ids=true, to_apply=%region_147.148 | all-reduce | flops 3 | bytes 24 | tf_op jit(solution)/shard_map/psum | solution.py:143
  242.3 1.7 collective-permute-start.35
  247.6 1.7 collective-permute-done.36
  249.3 2.8 collective-permute-done.37
  254.6 1.7 collective-permute-start.39
  259.9 1.8 collective-permute-done.40
  261.7 2.5 collective-permute-done.41
  265.9 30.4 %all-reduce.3 = (f32[1]{0:T(128)}, f32[1]{0:T(128)}, f32[1]{0:T(128)}) all-reduce(f32[1]{0:T(128)} %bitcast.335, f32[1]{0:T(128)} %bitcast.339, f32[1]{0:T(128)} %bitcast.340), channel_id=1, replica_groups=mesh['grp'=2,'zt'=4,'xy'=4] {'zt','xy'}, use_global_device_ids=true, to_apply=%region_185.186 | all-reduce | flops 3 | bytes 24 | tf_op jit(solution)/shard_map/psum | solution.py:143
  299.0 1.7 collective-permute-start.43
  304.5 1.7 collective-permute-done.44
  306.2 3.1 collective-permute-done.45
  311.8 1.7 collective-permute-start.47
  315.5 1.5 collective-permute-start.49
  317.0 2.0 collective-permute-done.48
  319.0 2.3 collective-permute-done.49
  323.1 30.6 %all-reduce.2 = (f32[1]{0:T(128)}, f32[1]{0:T(128)}, f32[1]{0:T(128)}) all-reduce(f32[1]{0:T(128)} %bitcast.400, f32[1]{0:T(128)} %bitcast.404, f32[1]{0:T(128)} %bitcast.405), channel_id=1, replica_groups=mesh['grp'=2,'zt'=4,'xy'=4] {'zt','xy'}, use_global_device_ids=true, to_apply=%region_223.224 | all-reduce | flops 3 | bytes 24 | tf_op jit(solution)/shard_map/psum | solution.py:143
  356.4 1.7 collective-permute-start.51
  361.8 1.5 collective-permute-done.52
  363.4 2.8 collective-permute-done.53
  368.7 1.7 collective-permute-start.55
  373.9 1.8 collective-permute-done.56
  375.7 2.5 collective-permute-done.57
  380.0 30.4 %all-reduce.1 = (f32[1]{0:T(128)}, f32[1]{0:T(128)}, f32[1]{0:T(128)}) all-reduce(f32[1]{0:T(128)} %bitcast.465, f32[1]{0:T(128)} %bitcast.469, f32[1]{0:T(128)} %bitcast.470), channel_id=1, replica_groups=mesh['grp'=2,'zt'=4,'xy'=4] {'zt','xy'}, use_global_device_ids=true, to_apply=%region_261.262 | all-reduce | flops 3 | bytes 24 | tf_op jit(solution)/shard_map/psum | solution.py:143
  413.1 1.7 collective-permute-start.59
  418.5 1.7 collective-permute-done.60
  420.2 3.1 collective-permute-done.61
  425.8 1.6 collective-permute-start.63
  429.4 1.5 collective-permute-start.65
  430.9 2.0 collective-permute-done.64
  432.9 2.3 collective-permute-done.65
  437.0 30.6 %psum.185 = f32[1]{0:T(128)} all-reduce(f32[1]{0:T(128)} %bitcast.531), channel_id=1, replica_groups=mesh['grp'=2,'zt'=4,'xy'=4] {'zt','xy'}, use_global_device_ids=true, to_apply=%region_299.300 | all-reduce | flops 1 | bytes 8 | tf_op jit(solution)/shard_map/psum | solution.py:143
  469.9 40.5 %psum.186 = f32[]{:T(128)} all-reduce(f32[]{:T(128)} %multiply_reduce_fusion.1), channel_id=1, replica_groups=mesh['grp'=2,'zt'=4,'xy'=4] {'grp','zt','xy'}, use_global_device_ids=true, to_apply=%region_302.303 | all-reduce | flops 1 | bytes 8 | tf_op jit(solution)/shard_map/psum | solution.py:172
  (699 shorter events, 87.5 us)
Async XLA Ops:
  8.8 13.1 %collective-permute-start = (f32[2,3,3,1,4,128]{5,4,3,2,1,0:T(4,128)S(1)}, f32[2,3,3,1,4,128]{5,4,3,2,1,0:T(4,128)S(1)}, u32[]{:S(2)}, u32[]{:S(2)}) collective-permute-start(f32[2,3,3,1,4,128]{5,4,3,2,1,0:T(4,128)S(1)} %slice.3115), channel_id=1, source_target_pairs={{3,0},{0,1},{1,2},{2,3},{7,4},{4,5},{5,6},{6,7},{11,8},{8,9},{9,10... | collective-permute-start | bytes 110600 | tf_op jit(solution)/shard_map/ppermute | solution.py:14
  10.7 11.4 %collective-permute-start.1 = (f32[2,3,3,2,1,128]{5,4,3,2,1,0:T(1,128)S(1)}, f32[2,3,3,2,1,128]{5,4,3,2,1,0:T(1,128)S(1)}, u32[]{:S(2)}, u32[]{:S(2)}) collective-permute-start(f32[2,3,3,2,1,128]{5,4,3,2,1,0:T(1,128)S(1)} %slice.3117), channel_id=1, source_target_pairs={{12,0},{0,4},{4,8},{8,12},{13,1},{1,5},{5,9},{9,13},{14,2},{2,6},{... | collective-permute-start | bytes 55304 | tf_op jit(solution)/shard_map/ppermute | solution.py:14
  10.8 3.3 collective-permute-start.2
  14.1 3.9 collective-permute-start.4
  16.2 5.6 %collective-permute-start.5 = (f32[1,2,3,1,6,128]{5,4,3,2,1,0:T(8,128)S(1)}, f32[1,2,3,1,6,128]{5,4,3,2,1,0:T(8,128)S(1)}, u32[]{:S(2)}, u32[]{:S(2)}) collective-permute-start(f32[1,2,3,1,6,128]{5,4,3,2,1,0:T(8,128)S(1)} %get-tuple-element.617), channel_id=1, source_target_pairs={{0,1},{1,2},{2,3},{3,0},{4,5},{5,6},{6,7},{7,4},{8,9},{9,10},{10,1... | collective-permute-start | bytes 55304 | tf_op jit(solution)/shard_map/ppermute | solution.py:23
  24.7 3.1 collective-permute-start.6
  27.9 3.9 collective-permute-start.8
  28.6 5.8 %collective-permute-start.9 = (f32[1,2,3,1,6,128]{5,4,3,2,1,0:T(8,128)S(1)}, f32[1,2,3,1,6,128]{5,4,3,2,1,0:T(8,128)S(1)}, u32[]{:S(2)}, u32[]{:S(2)}) collective-permute-start(f32[1,2,3,1,6,128]{5,4,3,2,1,0:T(8,128)S(1)} %get-tuple-element.613), channel_id=1, source_target_pairs={{0,1},{1,2},{2,3},{3,0},{4,5},{5,6},{6,7},{7,4},{8,9},{9,10},{10,1... | collective-permute-start | bytes 55304 | tf_op jit(solution)/shard_map/ppermute | solution.py:23
  71.3 3.1 collective-permute-start.10
  71.4 3.1 collective-permute-start.11
  74.5 3.9 collective-permute-start.12
  75.5 5.8 %collective-permute-start.13 = (f32[1,2,3,1,6,128]{5,4,3,2,1,0:T(8,128)S(1)}, f32[1,2,3,1,6,128]{5,4,3,2,1,0:T(8,128)S(1)}, u32[]{:S(2)}, u32[]{:S(2)}) collective-permute-start(f32[1,2,3,1,6,128]{5,4,3,2,1,0:T(8,128)S(1)} %get-tuple-element.609), channel_id=1, source_target_pairs={{0,1},{1,2},{2,3},{3,0},{4,5},{5,6},{6,7},{7,4},{8,9},{9,10},{10,1... | collective-permute-start | bytes 55304 | tf_op jit(solution)/shard_map/ppermute | solution.py:23
  83.8 3.1 collective-permute-start.14
  83.9 3.0 collective-permute-start.15
  87.0 4.1 collective-permute-start.16
  87.6 5.8 %collective-permute-start.17 = (f32[1,2,3,1,6,128]{5,4,3,2,1,0:T(8,128)S(1)}, f32[1,2,3,1,6,128]{5,4,3,2,1,0:T(8,128)S(1)}, u32[]{:S(2)}, u32[]{:S(2)}) collective-permute-start(f32[1,2,3,1,6,128]{5,4,3,2,1,0:T(8,128)S(1)} %get-tuple-element.605), channel_id=1, source_target_pairs={{0,1},{1,2},{2,3},{3,0},{4,5},{5,6},{6,7},{7,4},{8,9},{9,10},{10,1... | collective-permute-start | bytes 55304 | tf_op jit(solution)/shard_map/ppermute | solution.py:23
  128.3 3.1 collective-permute-start.18
  128.4 3.1 collective-permute-start.19
  131.5 3.9 collective-permute-start.20
  132.5 5.6 %collective-permute-start.21 = (f32[1,2,3,1,6,128]{5,4,3,2,1,0:T(8,128)S(1)}, f32[1,2,3,1,6,128]{5,4,3,2,1,0:T(8,128)S(1)}, u32[]{:S(2)}, u32[]{:S(2)}) collective-permute-start(f32[1,2,3,1,6,128]{5,4,3,2,1,0:T(8,128)S(1)} %get-tuple-element.601), channel_id=1, source_target_pairs={{0,1},{1,2},{2,3},{3,0},{4,5},{5,6},{6,7},{7,4},{8,9},{9,10},{10,1... | collective-permute-start | bytes 55304 | tf_op jit(solution)/shard_map/ppermute | solution.py:23
  140.7 3.1 collective-permute-start.22
  140.7 3.1 collective-permute-start.23
  143.8 3.9 collective-permute-start.24
  144.6 5.6 %collective-permute-start.25 = (f32[1,2,3,1,6,128]{5,4,3,2,1,0:T(8,128)S(1)}, f32[1,2,3,1,6,128]{5,4,3,2,1,0:T(8,128)S(1)}, u32[]{:S(2)}, u32[]{:S(2)}) collective-permute-start(f32[1,2,3,1,6,128]{5,4,3,2,1,0:T(8,128)S(1)} %get-tuple-element.597), channel_id=1, source_target_pairs={{0,1},{1,2},{2,3},{3,0},{4,5},{5,6},{6,7},{7,4},{8,9},{9,10},{10,1... | collective-permute-start | bytes 55304 | tf_op jit(solution)/shard_map/ppermute | solution.py:23
  185.0 3.1 collective-permute-start.26
  185.1 3.1 collective-permute-start.27
  188.2 4.1 collective-permute-start.28
  189.4 5.8 %collective-permute-start.29 = (f32[1,2,3,1,6,128]{5,4,3,2,1,0:T(8,128)S(1)}, f32[1,2,3,1,6,128]{5,4,3,2,1,0:T(8,128)S(1)}, u32[]{:S(2)}, u32[]{:S(2)}) collective-permute-start(f32[1,2,3,1,6,128]{5,4,3,2,1,0:T(8,128)S(1)} %get-tuple-element.593), channel_id=1, source_target_pairs={{0,1},{1,2},{2,3},{3,0},{4,5},{5,6},{6,7},{7,4},{8,9},{9,10},{10,1... | collective-permute-start | bytes 55304 | tf_op jit(solution)/shard_map/ppermute | solution.py:23
  197.8 3.1 collective-permute-start.30
  197.9 3.0 collective-permute-start.31
  200.9 4.1 collective-permute-start.32
  201.5 5.9 %collective-permute-start.33 = (f32[1,2,3,1,6,128]{5,4,3,2,1,0:T(8,128)S(1)}, f32[1,2,3,1,6,128]{5,4,3,2,1,0:T(8,128)S(1)}, u32[]{:S(2)}, u32[]{:S(2)}) collective-permute-start(f32[1,2,3,1,6,128]{5,4,3,2,1,0:T(8,128)S(1)} %get-tuple-element.589), channel_id=1, source_target_pairs={{0,1},{1,2},{2,3},{3,0},{4,5},{5,6},{6,7},{7,4},{8,9},{9,10},{10,1... | collective-permute-start | bytes 55304 | tf_op jit(solution)/shard_map/ppermute | solution.py:23
  242.3 3.1 collective-permute-start.34
  242.3 3.1 collective-permute-start.35
  245.4 3.9 collective-permute-start.36
  246.5 5.6 %collective-permute-start.37 = (f32[1,2,3,1,6,128]{5,4,3,2,1,0:T(8,128)S(1)}, f32[1,2,3,1,6,128]{5,4,3,2,1,0:T(8,128)S(1)}, u32[]{:S(2)}, u32[]{:S(2)}) collective-permute-start(f32[1,2,3,1,6,128]{5,4,3,2,1,0:T(8,128)S(1)} %get-tuple-element.585), channel_id=1, source_target_pairs={{0,1},{1,2},{2,3},{3,0},{4,5},{5,6},{6,7},{7,4},{8,9},{9,10},{10,1... | collective-permute-start | bytes 55304 | tf_op jit(solution)/shard_map/ppermute | solution.py:23
  254.6 3.1 collective-permute-start.38
  254.6 3.1 collective-permute-start.39
  257.8 3.9 collective-permute-start.40
  258.6 5.6 %collective-permute-start.41 = (f32[1,2,3,1,6,128]{5,4,3,2,1,0:T(8,128)S(1)}, f32[1,2,3,1,6,128]{5,4,3,2,1,0:T(8,128)S(1)}, u32[]{:S(2)}, u32[]{:S(2)}) collective-permute-start(f32[1,2,3,1,6,128]{5,4,3,2,1,0:T(8,128)S(1)} %get-tuple-element.581), channel_id=1, source_target_pairs={{0,1},{1,2},{2,3},{3,0},{4,5},{5,6},{6,7},{7,4},{8,9},{9,10},{10,1... | collective-permute-start | bytes 55304 | tf_op jit(solution)/shard_map/ppermute | solution.py:23
  298.9 3.1 collective-permute-start.42
  299.0 3.1 collective-permute-start.43
  302.1 4.1 collective-permute-start.44
  303.4 5.9 %collective-permute-start.45 = (f32[1,2,3,1,6,128]{5,4,3,2,1,0:T(8,128)S(1)}, f32[1,2,3,1,6,128]{5,4,3,2,1,0:T(8,128)S(1)}, u32[]{:S(2)}, u32[]{:S(2)}) collective-permute-start(f32[1,2,3,1,6,128]{5,4,3,2,1,0:T(8,128)S(1)} %get-tuple-element.577), channel_id=1, source_target_pairs={{0,1},{1,2},{2,3},{3,0},{4,5},{5,6},{6,7},{7,4},{8,9},{9,10},{10,1... | collective-permute-start | bytes 55304 | tf_op jit(solution)/shard_map/ppermute | solution.py:23
  311.8 3.1 collective-permute-start.46
  311.8 3.0 collective-permute-start.47
  314.9 4.1 collective-permute-start.48
  315.5 5.9 %collective-permute-start.49 = (f32[1,2,3,1,6,128]{5,4,3,2,1,0:T(8,128)S(1)}, f32[1,2,3,1,6,128]{5,4,3,2,1,0:T(8,128)S(1)}, u32[]{:S(2)}, u32[]{:S(2)}) collective-permute-start(f32[1,2,3,1,6,128]{5,4,3,2,1,0:T(8,128)S(1)} %get-tuple-element.573), channel_id=1, source_target_pairs={{0,1},{1,2},{2,3},{3,0},{4,5},{5,6},{6,7},{7,4},{8,9},{9,10},{10,1... | collective-permute-start | bytes 55304 | tf_op jit(solution)/shard_map/ppermute | solution.py:23
  356.3 3.1 collective-permute-start.50
  356.4 3.1 collective-permute-start.51
  359.5 3.9 collective-permute-start.52
  360.6 5.6 %collective-permute-start.53 = (f32[1,2,3,1,6,128]{5,4,3,2,1,0:T(8,128)S(1)}, f32[1,2,3,1,6,128]{5,4,3,2,1,0:T(8,128)S(1)}, u32[]{:S(2)}, u32[]{:S(2)}) collective-permute-start(f32[1,2,3,1,6,128]{5,4,3,2,1,0:T(8,128)S(1)} %get-tuple-element.569), channel_id=1, source_target_pairs={{0,1},{1,2},{2,3},{3,0},{4,5},{5,6},{6,7},{7,4},{8,9},{9,10},{10,1... | collective-permute-start | bytes 55304 | tf_op jit(solution)/shard_map/ppermute | solution.py:23
  368.7 3.1 collective-permute-start.54
  368.7 3.1 collective-permute-start.55
  371.8 3.9 collective-permute-start.56
  372.7 5.6 %collective-permute-start.57 = (f32[1,2,3,1,6,128]{5,4,3,2,1,0:T(8,128)S(1)}, f32[1,2,3,1,6,128]{5,4,3,2,1,0:T(8,128)S(1)}, u32[]{:S(2)}, u32[]{:S(2)}) collective-permute-start(f32[1,2,3,1,6,128]{5,4,3,2,1,0:T(8,128)S(1)} %get-tuple-element.565), channel_id=1, source_target_pairs={{0,1},{1,2},{2,3},{3,0},{4,5},{5,6},{6,7},{7,4},{8,9},{9,10},{10,1... | collective-permute-start | bytes 55304 | tf_op jit(solution)/shard_map/ppermute | solution.py:23
  413.0 3.1 collective-permute-start.58
  413.1 3.1 collective-permute-start.59
  416.2 4.0 collective-permute-start.60
  417.4 5.9 %collective-permute-start.61 = (f32[1,2,3,1,6,128]{5,4,3,2,1,0:T(8,128)S(1)}, f32[1,2,3,1,6,128]{5,4,3,2,1,0:T(8,128)S(1)}, u32[]{:S(2)}, u32[]{:S(2)}) collective-permute-start(f32[1,2,3,1,6,128]{5,4,3,2,1,0:T(8,128)S(1)} %get-tuple-element.559), channel_id=1, source_target_pairs={{0,1},{1,2},{2,3},{3,0},{4,5},{5,6},{6,7},{7,4},{8,9},{9,10},{10,1... | collective-permute-start | bytes 55304 | tf_op jit(solution)/shard_map/ppermute | solution.py:23
  425.7 3.1 collective-permute-start.62
  425.8 3.0 collective-permute-start.63
  428.8 4.1 collective-permute-start.64
  429.4 5.9 %collective-permute-start.65 = (f32[1,2,3,1,6,128]{5,4,3,2,1,0:T(8,128)S(1)}, f32[1,2,3,1,6,128]{5,4,3,2,1,0:T(8,128)S(1)}, u32[]{:S(2)}, u32[]{:S(2)}) collective-permute-start(f32[1,2,3,1,6,128]{5,4,3,2,1,0:T(8,128)S(1)} %get-tuple-element.555), channel_id=1, source_target_pairs={{0,1},{1,2},{2,3},{3,0},{4,5},{5,6},{6,7},{7,4},{8,9},{9,10},{10,1... | collective-permute-start | bytes 55304 | tf_op jit(solution)/shard_map/ppermute | solution.py:23
  (6 other events, 133.4 us)
where the time goes:
time: 513 us; the launch traced here: 512 us
  blocking collectives  293 us (57%)
  waiting for transfers between devices  89.2 us (17%)
  starting transfers between devices  64.4 us (13%)
  local copies, waits for them, and re-layouts  22.3 us (4%)
  between operations  22 us (4%)
  other arithmetic  21.7 us (4%)
    psum x7, blocking collectives, on_device(): lax.psum((local_dot(direction, image), local_dot(residual, image), local_...  214 us
    ppermute x32, waiting for transfers between devices, extended(): lax.ppermute(lax.slice_in_dim(block, block.shape[dim] - width, None, axis...  59.6 us
    ppermute x32, starting transfers between devices, extended(): lax.ppermute(lax.slice_in_dim(block, 0, width, axis=dim), axis, backward)  41.5 us
    psum x1, blocking collectives, on_device(): total = lax.psum(jnp.sum(source * rational), ('grp', 'zt', 'xy'))  40.5 us
    psum x1, blocking collectives, on_device(): norm_now = lax.psum(local_dot(source, source), ('zt', 'xy'))  30.7 us
    ppermute x32, waiting for transfers between devices, extended(): lax.ppermute(lax.slice_in_dim(block, 0, width, axis=dim), axis, backward)  29.6 us
    ppermute x32, starting transfers between devices, extended(): lax.ppermute(lax.slice_in_dim(block, block.shape[dim] - width, None, axis...  21 us
  transfers between devices with their start and end apart: 66, of which 47 were waited for; matrix products, arithmetic and copies ran while one was open for 1% of the time, Pallas kernels for 0%

commit v1 on v0

--- a/solution.py
+++ b/solution.py
@@ -132,7 +132,7 @@
     direction = source
     solutions = jnp.zeros((shifts.shape[0],) + source.shape, jnp.float32)
     directions = jnp.broadcast_to(source[None], solutions.shape)
-    norm_now = lax.psum(local_dot(source, source), ("zt", "xy"))
+    norm_now = lax.psum(lax.psum(local_dot(source, source), axis_name="zt"), axis_name="xy")
     zeta_now = jnp.ones((shifts.shape[0], members), jnp.float32)
     zeta_old = jnp.ones((shifts.shape[0], members), jnp.float32)
     alpha_old = jnp.ones((members,), jnp.float32)

time: 513 us -> 529 us (1.031)
  blocking collectives: 293 us -> 310 us
    psum x7 -> x8, blocking collectives: 214 us -> 245 us  [on_device(): lax.psum((local_dot(direction, image), local_dot(residual, image), local_...]
    psum x1 -> x2, blocking collectives: 30.7 us -> 16.4 us  [the longest x1 9.97 us: on_device(): lax.psum(lax.psum(local_dot(source, source), axis_name='zt'), axis_name='...]
where the time goes in v1:
time: 529 us; the launch traced here: 528 us
  blocking collectives  310 us (59%)
  waiting for transfers between devices  87.7 us (17%)
  starting transfers between devices  64.3 us (12%)
  local copies, waits for them, and re-layouts  22.3 us (4%)
  between operations  21.8 us (4%)
  other arithmetic  21.7 us (4%)
    psum x8, blocking collectives, on_device(): lax.psum((local_dot(direction, image), local_dot(residual, image), local_...  245 us
    ppermute x32, waiting for transfers between devices, extended(): lax.ppermute(lax.slice_in_dim(block, block.shape[dim] - width, None, axis...  58.4 us
    psum x1, blocking collectives, on_device(): total = lax.psum(jnp.sum(source * rational), ('grp', 'zt', 'xy'))  40.9 us
    ppermute x32, starting transfers between devices, extended(): lax.ppermute(lax.slice_in_dim(block, 0, width, axis=dim), axis, backward)  40.3 us
    ppermute x32, waiting for transfers between devices, extended(): lax.ppermute(lax.slice_in_dim(block, 0, width, axis=dim), axis, backward)  29.3 us
    ppermute x32, starting transfers between devices, extended(): lax.ppermute(lax.slice_in_dim(block, block.shape[dim] - width, None, axis...  22.2 us
  transfers between devices with their start and end apart: 66, of which 47 were waited for; matrix products, arithmetic and copies ran while one was open for 1% of the time, Pallas kernels for 0%

profile of v1, /device:TPU:0, one launch (start us, length us, event | category | flops | bytes accessed | tf_op | source)
XLA Modules:
  0.0 528.2 jit_solution(12589498465614910364)
XLA Ops:
  0.7 7.8 %all_gather.3 = f32[4,2,3,3,2,4,128]{6,5,4,3,2,1,0:T(4,128)S(1)} all-gather(f32[2,2,3,3,2,4,128]{6,5,4,3,2,1,0:T(4,128)} %param.10), channel_id=1, replica_groups=mesh['grp'=2,'zt'=4,'xy'=4] {'grp'}, dimensions={0}, use_global_device_ids=true | all-gather | bytes 442368 | tf_op jit(solution)/shard_map/all_gather | solution.py:112
  8.8 1.8 collective-permute-start
  10.8 1.6 collective-permute-start.2
  14.1 2.1 collective-permute-start.4
  16.3 1.7 collective-permute-done.4
  18.0 3.9 collective-permute-done.5
  24.9 1.6 collective-permute-start.7
  30.0 1.8 collective-permute-done.8
  31.7 2.6 collective-permute-done.9
  36.1 6.5 %psum.171 = f32[1]{0:T(128)} all-reduce(f32[1]{0:T(128)} %bitcast), channel_id=1, replica_groups=mesh['grp'=2,'zt'=4,'xy'=4] {'zt'}, use_global_device_ids=true, to_apply=%region_1.2 | all-reduce | flops 1 | bytes 8 | tf_op jit(solution)/shard_map/psum | solution.py:135
  42.6 10.0 %psum.172 = f32[1]{0:T(128)} all-reduce(f32[1]{0:T(128)} %psum.171), channel_id=1, replica_groups=mesh['grp'=2,'zt'=4,'xy'=4] {'xy'}, use_global_device_ids=true, to_apply=%region_2.3 | all-reduce | flops 1 | bytes 8 | tf_op jit(solution)/shard_map/psum | solution.py:135
  52.6 31.3 %all-reduce.7 = (f32[1]{0:T(128)}, f32[1]{0:T(128)}) all-reduce(f32[1]{0:T(128)} %bitcast.76, f32[1]{0:T(128)} %bitcast.80), channel_id=1, replica_groups=mesh['grp'=2,'zt'=4,'xy'=4] {'zt','xy'}, use_global_device_ids=true, to_apply=%region_36.37 | all-reduce | flops 2 | bytes 16 | tf_op jit(solution)/shard_map/psum | solution.py:143
  88.3 1.7 collective-permute-start.11
  91.7 1.8 collective-permute-start.13
  93.5 1.8 collective-permute-done.12
  95.3 2.1 collective-permute-done.13
  103.4 1.6 collective-permute-start.17
  105.1 1.8 collective-permute-done.16
  106.9 2.2 collective-permute-done.17
  110.8 30.8 %all-reduce.6 = (f32[1]{0:T(128)}, f32[1]{0:T(128)}, f32[1]{0:T(128)}) all-reduce(f32[1]{0:T(128)} %bitcast.140, f32[1]{0:T(128)} %bitcast.144, f32[1]{0:T(128)} %bitcast.145), channel_id=1, replica_groups=mesh['grp'=2,'zt'=4,'xy'=4] {'zt','xy'}, use_global_device_ids=true, to_apply=%region_72.73 | all-reduce | flops 3 | bytes 24 | tf_op jit(solution)/shard_map/psum | solution.py:143
  144.1 1.7 collective-permute-start.19
  149.4 1.8 collective-permute-done.20
  151.1 2.9 collective-permute-done.21
  156.5 1.7 collective-permute-start.23
  161.7 2.0 collective-permute-done.24
  163.7 2.4 collective-permute-done.25
  167.9 30.8 %all-reduce.5 = (f32[1]{0:T(128)}, f32[1]{0:T(128)}, f32[1]{0:T(128)}) all-reduce(f32[1]{0:T(128)} %bitcast.205, f32[1]{0:T(128)} %bitcast.209, f32[1]{0:T(128)} %bitcast.210), channel_id=1, replica_groups=mesh['grp'=2,'zt'=4,'xy'=4] {'zt','xy'}, use_global_device_ids=true, to_apply=%region_110.111 | all-reduce | flops 3 | bytes 24 | tf_op jit(solution)/shard_map/psum | solution.py:143
  201.3 1.7 collective-permute-start.27
  206.6 1.7 collective-permute-done.28
  208.3 2.8 collective-permute-done.29
  213.6 1.7 collective-permute-start.31
  218.9 1.8 collective-permute-done.32
  220.7 2.5 collective-permute-done.33
  225.0 30.4 %all-reduce.4 = (f32[1]{0:T(128)}, f32[1]{0:T(128)}, f32[1]{0:T(128)}) all-reduce(f32[1]{0:T(128)} %bitcast.270, f32[1]{0:T(128)} %bitcast.274, f32[1]{0:T(128)} %bitcast.275), channel_id=1, replica_groups=mesh['grp'=2,'zt'=4,'xy'=4] {'zt','xy'}, use_global_device_ids=true, to_apply=%region_148.149 | all-reduce | flops 3 | bytes 24 | tf_op jit(solution)/shard_map/psum | solution.py:143
  257.9 1.7 collective-permute-start.35
  263.4 1.7 collective-permute-done.36
  265.1 3.1 collective-permute-done.37
  270.8 1.7 collective-permute-start.39
  275.9 2.0 collective-permute-done.40
  277.9 2.3 collective-permute-done.41
  282.0 30.6 %all-reduce.3 = (f32[1]{0:T(128)}, f32[1]{0:T(128)}, f32[1]{0:T(128)}) all-reduce(f32[1]{0:T(128)} %bitcast.335, f32[1]{0:T(128)} %bitcast.339, f32[1]{0:T(128)} %bitcast.340), channel_id=1, replica_groups=mesh['grp'=2,'zt'=4,'xy'=4] {'zt','xy'}, use_global_device_ids=true, to_apply=%region_186.187 | all-reduce | flops 3 | bytes 24 | tf_op jit(solution)/shard_map/psum | solution.py:143
  315.3 1.7 collective-permute-start.43
  320.5 1.8 collective-permute-done.44
  322.3 2.8 collective-permute-done.45
  327.6 1.7 collective-permute-start.47
  332.8 1.8 collective-permute-done.48
  334.6 2.5 collective-permute-done.49
  339.0 30.4 %all-reduce.2 = (f32[1]{0:T(128)}, f32[1]{0:T(128)}, f32[1]{0:T(128)}) all-reduce(f32[1]{0:T(128)} %bitcast.400, f32[1]{0:T(128)} %bitcast.404, f32[1]{0:T(128)} %bitcast.405), channel_id=1, replica_groups=mesh['grp'=2,'zt'=4,'xy'=4] {'zt','xy'}, use_global_device_ids=true, to_apply=%region_224.225 | all-reduce | flops 3 | bytes 24 | tf_op jit(solution)/shard_map/psum | solution.py:143
  372.0 1.7 collective-permute-start.51
  377.7 1.5 collective-permute-done.52
  379.2 3.1 collective-permute-done.53
  384.8 1.7 collective-permute-start.55
  388.5 1.5 collective-permute-start.57
  390.0 2.0 collective-permute-done.56
  392.0 2.3 collective-permute-done.57
  396.1 30.6 %all-reduce.1 = (f32[1]{0:T(128)}, f32[1]{0:T(128)}, f32[1]{0:T(128)}) all-reduce(f32[1]{0:T(128)} %bitcast.465, f32[1]{0:T(128)} %bitcast.469, f32[1]{0:T(128)} %bitcast.470), channel_id=1, replica_groups=mesh['grp'=2,'zt'=4,'xy'=4] {'zt','xy'}, use_global_device_ids=true, to_apply=%region_262.263 | all-reduce | flops 3 | bytes 24 | tf_op jit(solution)/shard_map/psum | solution.py:143
  429.3 1.7 collective-permute-start.59
  434.5 1.8 collective-permute-done.60
  436.3 2.8 collective-permute-done.61
  441.5 1.7 collective-permute-start.63
  446.8 1.8 collective-permute-done.64
  448.6 2.5 collective-permute-done.65
  452.8 30.3 %psum.193 = f32[1]{0:T(128)} all-reduce(f32[1]{0:T(128)} %bitcast.531), channel_id=1, replica_groups=mesh['grp'=2,'zt'=4,'xy'=4] {'zt','xy'}, use_global_device_ids=true, to_apply=%region_300.301 | all-reduce | flops 1 | bytes 8 | tf_op jit(solution)/shard_map/psum | solution.py:143
  485.5 40.9 %psum.194 = f32[]{:T(128)} all-reduce(f32[]{:T(128)} %multiply_reduce_fusion.1), channel_id=1, replica_groups=mesh['grp'=2,'zt'=4,'xy'=4] {'grp','zt','xy'}, use_global_device_ids=true, to_apply=%region_303.304 | all-reduce | flops 1 | bytes 8 | tf_op jit(solution)/shard_map/psum | solution.py:172
  (701 shorter events, 90.0 us)
Async XLA Ops:
  8.8 13.1 %collective-permute-start = (f32[2,3,3,1,4,128]{5,4,3,2,1,0:T(4,128)S(1)}, f32[2,3,3,1,4,128]{5,4,3,2,1,0:T(4,128)S(1)}, u32[]{:S(2)}, u32[]{:S(2)}) collective-permute-start(f32[2,3,3,1,4,128]{5,4,3,2,1,0:T(4,128)S(1)} %slice.3115), channel_id=1, source_target_pairs={{3,0},{0,1},{1,2},{2,3},{7,4},{4,5},{5,6},{6,7},{11,8},{8,9},{9,10... | collective-permute-start | bytes 110600 | tf_op jit(solution)/shard_map/ppermute | solution.py:14
  10.7 11.4 %collective-permute-start.1 = (f32[2,3,3,2,1,128]{5,4,3,2,1,0:T(1,128)S(1)}, f32[2,3,3,2,1,128]{5,4,3,2,1,0:T(1,128)S(1)}, u32[]{:S(2)}, u32[]{:S(2)}) collective-permute-start(f32[2,3,3,2,1,128]{5,4,3,2,1,0:T(1,128)S(1)} %slice.3117), channel_id=1, source_target_pairs={{12,0},{0,4},{4,8},{8,12},{13,1},{1,5},{5,9},{9,13},{14,2},{2,6},{... | collective-permute-start | bytes 55304 | tf_op jit(solution)/shard_map/ppermute | solution.py:14
  10.8 3.3 collective-permute-start.2
  14.1 3.9 collective-permute-start.4
  16.2 5.6 %collective-permute-start.5 = (f32[1,2,3,1,6,128]{5,4,3,2,1,0:T(8,128)S(1)}, f32[1,2,3,1,6,128]{5,4,3,2,1,0:T(8,128)S(1)}, u32[]{:S(2)}, u32[]{:S(2)}) collective-permute-start(f32[1,2,3,1,6,128]{5,4,3,2,1,0:T(8,128)S(1)} %get-tuple-element.616), channel_id=1, source_target_pairs={{0,1},{1,2},{2,3},{3,0},{4,5},{5,6},{6,7},{7,4},{8,9},{9,10},{10,1... | collective-permute-start | bytes 55304 | tf_op jit(solution)/shard_map/ppermute | solution.py:23
  24.7 3.1 collective-permute-start.6
  24.9 2.9 collective-permute-start.7
  27.9 3.9 collective-permute-start.8
  28.6 5.8 %collective-permute-start.9 = (f32[1,2,3,1,6,128]{5,4,3,2,1,0:T(8,128)S(1)}, f32[1,2,3,1,6,128]{5,4,3,2,1,0:T(8,128)S(1)}, u32[]{:S(2)}, u32[]{:S(2)}) collective-permute-start(f32[1,2,3,1,6,128]{5,4,3,2,1,0:T(8,128)S(1)} %get-tuple-element.612), channel_id=1, source_target_pairs={{0,1},{1,2},{2,3},{3,0},{4,5},{5,6},{6,7},{7,4},{8,9},{9,10},{10,1... | collective-permute-start | bytes 55304 | tf_op jit(solution)/shard_map/ppermute | solution.py:23
  88.2 3.1 collective-permute-start.10
  88.3 3.1 collective-permute-start.11
  91.4 3.9 collective-permute-start.12
  91.7 5.6 %collective-permute-start.13 = (f32[1,2,3,1,6,128]{5,4,3,2,1,0:T(8,128)S(1)}, f32[1,2,3,1,6,128]{5,4,3,2,1,0:T(8,128)S(1)}, u32[]{:S(2)}, u32[]{:S(2)}) collective-permute-start(f32[1,2,3,1,6,128]{5,4,3,2,1,0:T(8,128)S(1)} %get-tuple-element.608), channel_id=1, source_target_pairs={{0,1},{1,2},{2,3},{3,0},{4,5},{5,6},{6,7},{7,4},{8,9},{9,10},{10,1... | collective-permute-start | bytes 55304 | tf_op jit(solution)/shard_map/ppermute | solution.py:23
  99.8 3.1 collective-permute-start.14
  103.0 3.9 collective-permute-start.16
  103.4 5.6 %collective-permute-start.17 = (f32[1,2,3,1,6,128]{5,4,3,2,1,0:T(8,128)S(1)}, f32[1,2,3,1,6,128]{5,4,3,2,1,0:T(8,128)S(1)}, u32[]{:S(2)}, u32[]{:S(2)}) collective-permute-start(f32[1,2,3,1,6,128]{5,4,3,2,1,0:T(8,128)S(1)} %get-tuple-element.604), channel_id=1, source_target_pairs={{0,1},{1,2},{2,3},{3,0},{4,5},{5,6},{6,7},{7,4},{8,9},{9,10},{10,1... | collective-permute-start | bytes 55304 | tf_op jit(solution)/shard_map/ppermute | solution.py:23
  144.1 3.1 collective-permute-start.18
  144.1 3.1 collective-permute-start.19
  147.3 3.9 collective-permute-start.20
  148.2 5.8 %collective-permute-start.21 = (f32[1,2,3,1,6,128]{5,4,3,2,1,0:T(8,128)S(1)}, f32[1,2,3,1,6,128]{5,4,3,2,1,0:T(8,128)S(1)}, u32[]{:S(2)}, u32[]{:S(2)}) collective-permute-start(f32[1,2,3,1,6,128]{5,4,3,2,1,0:T(8,128)S(1)} %get-tuple-element.600), channel_id=1, source_target_pairs={{0,1},{1,2},{2,3},{3,0},{4,5},{5,6},{6,7},{7,4},{8,9},{9,10},{10,1... | collective-permute-start | bytes 55304 | tf_op jit(solution)/shard_map/ppermute | solution.py:23
  156.5 3.1 collective-permute-start.22
  156.5 3.1 collective-permute-start.23
  159.6 4.1 collective-permute-start.24
  160.3 5.8 %collective-permute-start.25 = (f32[1,2,3,1,6,128]{5,4,3,2,1,0:T(8,128)S(1)}, f32[1,2,3,1,6,128]{5,4,3,2,1,0:T(8,128)S(1)}, u32[]{:S(2)}, u32[]{:S(2)}) collective-permute-start(f32[1,2,3,1,6,128]{5,4,3,2,1,0:T(8,128)S(1)} %get-tuple-element.596), channel_id=1, source_target_pairs={{0,1},{1,2},{2,3},{3,0},{4,5},{5,6},{6,7},{7,4},{8,9},{9,10},{10,1... | collective-permute-start | bytes 55304 | tf_op jit(solution)/shard_map/ppermute | solution.py:23
  201.2 3.1 collective-permute-start.26
  201.3 3.1 collective-permute-start.27
  204.4 3.9 collective-permute-start.28
  205.5 5.6 %collective-permute-start.29 = (f32[1,2,3,1,6,128]{5,4,3,2,1,0:T(8,128)S(1)}, f32[1,2,3,1,6,128]{5,4,3,2,1,0:T(8,128)S(1)}, u32[]{:S(2)}, u32[]{:S(2)}) collective-permute-start(f32[1,2,3,1,6,128]{5,4,3,2,1,0:T(8,128)S(1)} %get-tuple-element.592), channel_id=1, source_target_pairs={{0,1},{1,2},{2,3},{3,0},{4,5},{5,6},{6,7},{7,4},{8,9},{9,10},{10,1... | collective-permute-start | bytes 55304 | tf_op jit(solution)/shard_map/ppermute | solution.py:23
  213.6 3.1 collective-permute-start.30
  213.6 3.1 collective-permute-start.31
  216.8 3.9 collective-permute-start.32
  217.6 5.6 %collective-permute-start.33 = (f32[1,2,3,1,6,128]{5,4,3,2,1,0:T(8,128)S(1)}, f32[1,2,3,1,6,128]{5,4,3,2,1,0:T(8,128)S(1)}, u32[]{:S(2)}, u32[]{:S(2)}) collective-permute-start(f32[1,2,3,1,6,128]{5,4,3,2,1,0:T(8,128)S(1)} %get-tuple-element.588), channel_id=1, source_target_pairs={{0,1},{1,2},{2,3},{3,0},{4,5},{5,6},{6,7},{7,4},{8,9},{9,10},{10,1... | collective-permute-start | bytes 55304 | tf_op jit(solution)/shard_map/ppermute | solution.py:23
  257.9 3.1 collective-permute-start.34
  257.9 3.1 collective-permute-start.35
  261.1 4.1 collective-permute-start.36
  262.3 5.8 %collective-permute-start.37 = (f32[1,2,3,1,6,128]{5,4,3,2,1,0:T(8,128)S(1)}, f32[1,2,3,1,6,128]{5,4,3,2,1,0:T(8,128)S(1)}, u32[]{:S(2)}, u32[]{:S(2)}) collective-permute-start(f32[1,2,3,1,6,128]{5,4,3,2,1,0:T(8,128)S(1)} %get-tuple-element.584), channel_id=1, source_target_pairs={{0,1},{1,2},{2,3},{3,0},{4,5},{5,6},{6,7},{7,4},{8,9},{9,10},{10,1... | collective-permute-start | bytes 55304 | tf_op jit(solution)/shard_map/ppermute | solution.py:23
  270.7 3.1 collective-permute-start.38
  270.8 3.0 collective-permute-start.39
  273.8 4.1 collective-permute-start.40
  274.4 5.9 %collective-permute-start.41 = (f32[1,2,3,1,6,128]{5,4,3,2,1,0:T(8,128)S(1)}, f32[1,2,3,1,6,128]{5,4,3,2,1,0:T(8,128)S(1)}, u32[]{:S(2)}, u32[]{:S(2)}) collective-permute-start(f32[1,2,3,1,6,128]{5,4,3,2,1,0:T(8,128)S(1)} %get-tuple-element.580), channel_id=1, source_target_pairs={{0,1},{1,2},{2,3},{3,0},{4,5},{5,6},{6,7},{7,4},{8,9},{9,10},{10,1... | collective-permute-start | bytes 55304 | tf_op jit(solution)/shard_map/ppermute | solution.py:23
  315.2 3.1 collective-permute-start.42
  315.3 3.1 collective-permute-start.43
  318.4 3.9 collective-permute-start.44
  319.5 5.6 %collective-permute-start.45 = (f32[1,2,3,1,6,128]{5,4,3,2,1,0:T(8,128)S(1)}, f32[1,2,3,1,6,128]{5,4,3,2,1,0:T(8,128)S(1)}, u32[]{:S(2)}, u32[]{:S(2)}) collective-permute-start(f32[1,2,3,1,6,128]{5,4,3,2,1,0:T(8,128)S(1)} %get-tuple-element.576), channel_id=1, source_target_pairs={{0,1},{1,2},{2,3},{3,0},{4,5},{5,6},{6,7},{7,4},{8,9},{9,10},{10,1... | collective-permute-start | bytes 55304 | tf_op jit(solution)/shard_map/ppermute | solution.py:23
  327.6 3.1 collective-permute-start.46
  327.6 3.1 collective-permute-start.47
  330.7 3.9 collective-permute-start.48
  331.6 5.6 %collective-permute-start.49 = (f32[1,2,3,1,6,128]{5,4,3,2,1,0:T(8,128)S(1)}, f32[1,2,3,1,6,128]{5,4,3,2,1,0:T(8,128)S(1)}, u32[]{:S(2)}, u32[]{:S(2)}) collective-permute-start(f32[1,2,3,1,6,128]{5,4,3,2,1,0:T(8,128)S(1)} %get-tuple-element.572), channel_id=1, source_target_pairs={{0,1},{1,2},{2,3},{3,0},{4,5},{5,6},{6,7},{7,4},{8,9},{9,10},{10,1... | collective-permute-start | bytes 55304 | tf_op jit(solution)/shard_map/ppermute | solution.py:23
  371.9 3.1 collective-permute-start.50
  372.0 3.1 collective-permute-start.51
  375.1 4.1 collective-permute-start.52
  376.4 5.8 %collective-permute-start.53 = (f32[1,2,3,1,6,128]{5,4,3,2,1,0:T(8,128)S(1)}, f32[1,2,3,1,6,128]{5,4,3,2,1,0:T(8,128)S(1)}, u32[]{:S(2)}, u32[]{:S(2)}) collective-permute-start(f32[1,2,3,1,6,128]{5,4,3,2,1,0:T(8,128)S(1)} %get-tuple-element.568), channel_id=1, source_target_pairs={{0,1},{1,2},{2,3},{3,0},{4,5},{5,6},{6,7},{7,4},{8,9},{9,10},{10,1... | collective-permute-start | bytes 55304 | tf_op jit(solution)/shard_map/ppermute | solution.py:23
  384.7 3.1 collective-permute-start.54
  384.8 3.0 collective-permute-start.55
  387.9 4.1 collective-permute-start.56
  388.5 5.9 %collective-permute-start.57 = (f32[1,2,3,1,6,128]{5,4,3,2,1,0:T(8,128)S(1)}, f32[1,2,3,1,6,128]{5,4,3,2,1,0:T(8,128)S(1)}, u32[]{:S(2)}, u32[]{:S(2)}) collective-permute-start(f32[1,2,3,1,6,128]{5,4,3,2,1,0:T(8,128)S(1)} %get-tuple-element.564), channel_id=1, source_target_pairs={{0,1},{1,2},{2,3},{3,0},{4,5},{5,6},{6,7},{7,4},{8,9},{9,10},{10,1... | collective-permute-start | bytes 55304 | tf_op jit(solution)/shard_map/ppermute | solution.py:23
  429.2 3.1 collective-permute-start.58
  429.3 3.1 collective-permute-start.59
  432.4 3.9 collective-permute-start.60
  433.5 5.6 %collective-permute-start.61 = (f32[1,2,3,1,6,128]{5,4,3,2,1,0:T(8,128)S(1)}, f32[1,2,3,1,6,128]{5,4,3,2,1,0:T(8,128)S(1)}, u32[]{:S(2)}, u32[]{:S(2)}) collective-permute-start(f32[1,2,3,1,6,128]{5,4,3,2,1,0:T(8,128)S(1)} %get-tuple-element.558), channel_id=1, source_target_pairs={{0,1},{1,2},{2,3},{3,0},{4,5},{5,6},{6,7},{7,4},{8,9},{9,10},{10,1... | collective-permute-start | bytes 55304 | tf_op jit(solution)/shard_map/ppermute | solution.py:23
  441.5 3.1 collective-permute-start.62
  441.5 3.1 collective-permute-start.63
  444.6 3.9 collective-permute-start.64
  445.5 5.6 %collective-permute-start.65 = (f32[1,2,3,1,6,128]{5,4,3,2,1,0:T(8,128)S(1)}, f32[1,2,3,1,6,128]{5,4,3,2,1,0:T(8,128)S(1)}, u32[]{:S(2)}, u32[]{:S(2)}) collective-permute-start(f32[1,2,3,1,6,128]{5,4,3,2,1,0:T(8,128)S(1)} %get-tuple-element.554), channel_id=1, source_target_pairs={{0,1},{1,2},{2,3},{3,0},{4,5},{5,6},{6,7},{7,4},{8,9},{9,10},{10,1... | collective-permute-start | bytes 55304 | tf_op jit(solution)/shard_map/ppermute | solution.py:23
  (6 other events, 133.6 us)
